TPU v7x, 32 devices: a whole 2x2x4 slice. The times are simulated.
32 devices in a mesh: groups: 1, expert: 16 (over z, y, x), replica: 2 (over core).
Axes of the slice: x: 2, y: 2, z: 4, core: 2. Of those that a mesh axis runs over, the one named last changes fastest.
Arguments:
- queries: bfloat16 [128, 8192], P(('groups', 'expert', 'replica')), may hold values from -250 to 250
- token_keys: bfloat16 [128, 512], P(('groups', 'expert', 'replica')), may hold values from -6 to 6
- token_values: bfloat16 [128, 512], P(('groups', 'expert', 'replica')), may hold values from -6 to 6
- stored_keys: bfloat16 [128, 256, 512], P(('groups', 'expert', 'replica')), may hold values from -7 to 7
- stored_values: bfloat16 [128, 256, 512], P(('groups', 'expert', 'replica')), may hold values from -6 to 6
- kv_len: int32 [128], P(('groups', 'expert', 'replica')), may hold values from 2 to 256, as said below
- residual: bfloat16 [128, 4096], P(('groups', 'expert', 'replica')), may hold values from -6 to 6
- out_weight: bfloat16 [8192, 4096], P(('expert', 'replica')), may hold values from -0.1875 to 0.1875
- norm_gain: bfloat16 [4096], replicated, may hold values from 0.25 to 1.75
- expert_ids: int32 [128, 8], P(('groups', 'expert')), may hold values from 0 to 15, all different within a row; in each aligned block of 8 rows (0 to 7, 8 to 15, ...) at most 4 rows name the same one
- route_weight: float32 [128, 8], P(('groups', 'expert')), may hold values from 0.05 to 1
- w_gate: bfloat16 [16, 4096, 768], P('expert', None, 'replica'), may hold values from -0.09375 to 0.09375
- w_up: bfloat16 [16, 4096, 768], P('expert', None, 'replica'), may hold values from -0.09375 to 0.09375
- w_down: bfloat16 [16, 768, 4096], P('expert', 'replica'), may hold values from -0.4375 to 0.4375
Outputs:
- updated: bfloat16 [128, 4096], P(('groups', 'expert', 'replica'))
Inputs may be any that keep to these rules, and one draw needn't show every extreme that they name: `kv_len`: at least 2; some sequence uses all 256 positions. `expert_ids`: each token names 8 different experts; in each aligned block of 8 tokens no expert is named by more than 4 tokens, and some block reaches it.
All inputs are finite; a program needn't handle non-finite values.
Results may differ from a plain program's by a relative error of at most 0.01.
Values may be sent and summed in bfloat16 or wider, within the bound.
A program may use at most 64 MiB of HBM per device.

v0:
```python
import math
import jax
import jax.numpy as jnp
from jax import lax
from jax.sharding import PartitionSpec as P

HEAD_WIDTH = 128


def shifted(block, axis, distance):
    devices = range(lax.axis_size(axis))
    route = [(i - distance, i) for i in devices if i - distance in devices]
    return lax.ppermute(block, axis, route)


def attend_local(queries, token_keys, token_values, stored_keys, stored_values, kv_len):
    seq_count = queries.shape[0]
    cache_len = stored_keys.shape[1]
    kv_count = token_keys.shape[1] // HEAD_WIDTH
    query_group_width = queries.shape[1] // HEAD_WIDTH // kv_count
    query_head_rows = queries.reshape(seq_count, kv_count, query_group_width, HEAD_WIDTH)
    keys_from_cache = stored_keys.reshape(seq_count, cache_len, kv_count, HEAD_WIDTH)
    values_from_cache = stored_values.reshape(seq_count, cache_len, kv_count, HEAD_WIDTH)
    keys_latest = token_keys.reshape(seq_count, kv_count, HEAD_WIDTH)
    values_latest = token_values.astype(jnp.float32).reshape(seq_count, kv_count, HEAD_WIDTH)
    inv_root = 1.0 / math.sqrt(HEAD_WIDTH)
    cached_scores = (
        jnp.einsum(
            "bgqd,bpgd->bgqp", query_head_rows, keys_from_cache, preferred_element_type=jnp.float32
        )
        * inv_root
    )
    positions = lax.broadcasted_iota(jnp.int32, (seq_count, cache_len), 1)
    visible = positions < kv_len[:, None]
    cached_scores = jnp.where(visible[:, None, None, :], cached_scores, -jnp.inf)
    fresh_score = (
        jnp.einsum(
            "bgqd,bgd->bgq", query_head_rows, keys_latest, preferred_element_type=jnp.float32
        )
        * inv_root
    )
    highest = jnp.maximum(jnp.max(cached_scores, axis=-1), fresh_score)
    cached_exp = jnp.exp(cached_scores - highest[..., None])
    fresh_exp = jnp.exp(fresh_score - highest)
    totals = jnp.sum(cached_exp, axis=-1) + fresh_exp
    cached_prob = (cached_exp / totals[..., None]).astype(jnp.bfloat16)
    fresh_prob = lax.optimization_barrier((fresh_exp / totals).astype(jnp.bfloat16)).astype(
        jnp.float32
    )
    mixed = jnp.einsum(
        "bgqp,bpgd->bgqd", cached_prob, values_from_cache, preferred_element_type=jnp.float32
    )
    mixed = mixed + fresh_prob[..., None] * values_latest[:, :, None, :]
    return mixed.reshape(seq_count, -1).astype(jnp.bfloat16)


def on_device(
    queries,
    token_keys,
    token_values,
    stored_keys,
    stored_values,
    kv_len,
    residual,
    out_weight,
    norm_gain,
    expert_ids,
    route_weight,
    w_gate,
    w_up,
    w_down,
):
    attended = attend_local(queries, token_keys, token_values, stored_keys, stored_values, kv_len)
    column_groups = 8
    device_count = lax.axis_size(("expert", "replica"))
    seq_count, feature_total = attended.shape
    row_count, model_width = out_weight.shape
    feature_groups = device_count // column_groups
    feature_block = feature_total // feature_groups
    col_width = model_width // column_groups
    device_rank = lax.axis_index(("expert", "replica"))
    block_place = device_rank % column_groups
    slot_ids = jnp.arange(column_groups, dtype=jnp.int32)
    own_piece = lax.dynamic_slice_in_dim(out_weight, block_place * col_width, col_width, 1)
    empty_block = jnp.zeros((column_groups, row_count, col_width), out_weight.dtype)
    stacked = jnp.where((slot_ids == block_place)[:, None, None], own_piece[None], empty_block)
    for offset in range(1 - column_groups, column_groups):
        if offset != 0:
            target_place = (device_rank + offset) % column_groups
            sent_piece = lax.dynamic_slice_in_dim(
                out_weight, target_place * col_width, col_width, 1
            )
            arrived_piece = shifted(sent_piece, ("expert", "replica"), offset)
            stacked = jnp.where(
                (slot_ids == block_place - offset)[:, None, None], arrived_piece[None], stacked
            )
    weight_block = stacked.reshape(column_groups * row_count, col_width)
    repeated = jnp.repeat(
        attended.reshape(seq_count, feature_groups, feature_block), column_groups, axis=1
    )
    all_tokens = lax.all_to_all(
        repeated, ("expert", "replica"), split_axis=1, concat_axis=0, tiled=True
    )
    all_tokens = all_tokens.reshape(-1, feature_block)
    partial_cols = jnp.dot(all_tokens, weight_block, preferred_element_type=jnp.float32)
    partial_cols = partial_cols.reshape(-1, 1, col_width)
    came_back = lax.all_to_all(
        partial_cols.astype(jnp.bfloat16),
        ("expert", "replica"),
        split_axis=0,
        concat_axis=1,
        tiled=True,
    ).astype(partial_cols.dtype)
    projected = jnp.sum(
        came_back.reshape(seq_count, feature_groups, column_groups, col_width), axis=1
    ).reshape(seq_count, model_width)
    hidden_state = residual.astype(jnp.float32) + projected
    mean_square = jnp.mean(hidden_state * hidden_state, axis=-1, keepdims=True)
    normed = (hidden_state * lax.rsqrt(mean_square + 1e-06) * norm_gain.astype(jnp.float32)).astype(
        jnp.bfloat16
    )
    pair_tokens = lax.all_gather(normed, "replica", axis=0, tiled=True)
    token_count, topk_count = expert_ids.shape
    expert_count = lax.axis_size("expert")
    capacity = max(2, -(-(token_count * topk_count) // expert_count))
    flat_ids = expert_ids.reshape(-1)
    row_total = flat_ids.shape[0]
    same_expert = flat_ids[:, None] == flat_ids[None, :]
    row_iota = lax.broadcasted_iota(jnp.int32, (row_total, row_total), 0)
    col_iota = lax.broadcasted_iota(jnp.int32, (row_total, row_total), 1)
    slot_ranks = jnp.sum(jnp.where(same_expert & (col_iota < row_iota), 1, 0), axis=1).astype(
        jnp.int32
    )
    slot_of = (flat_ids * capacity + slot_ranks).reshape(token_count, topk_count)
    slot_total = expert_count * capacity
    slot_iota = jnp.arange(slot_total, dtype=jnp.int32)
    slot_hits = slot_of[None, :, :] == slot_iota[:, None, None]
    pick_table = jnp.sum(slot_hits.astype(jnp.float32), axis=2).astype(jnp.bfloat16)
    outgoing = jnp.dot(pick_table, pair_tokens, preferred_element_type=jnp.float32).astype(
        jnp.bfloat16
    )
    outgoing = outgoing.reshape(expert_count, capacity, -1)
    mixing = route_weight / jnp.sum(route_weight, axis=1, keepdims=True)
    combine_rows = jnp.sum(jnp.where(slot_hits, mixing[None, :, :], 0.0), axis=2).T
    incoming = lax.all_to_all(outgoing, "expert", split_axis=0, concat_axis=0, tiled=True)
    model_width = incoming.shape[-1]
    lead_shape = incoming.shape[:2]
    slot_rows = incoming.reshape(-1, model_width)
    gate_act = jnp.dot(slot_rows, w_gate[0], preferred_element_type=jnp.float32)
    up_act = jnp.dot(slot_rows, w_up[0], preferred_element_type=jnp.float32)
    hidden_act = (jax.nn.silu(gate_act) * up_act).astype(jnp.bfloat16)
    partial_value = jnp.dot(hidden_act, w_down[0], preferred_element_type=jnp.float32).reshape(
        lead_shape + (model_width,)
    )
    summed_halves = lax.psum(partial_value.astype(jnp.bfloat16), "replica").astype(jnp.float32)
    arrived = lax.all_to_all(
        summed_halves.astype(jnp.bfloat16), "expert", split_axis=0, concat_axis=0, tiled=True
    ).astype(summed_halves.dtype)
    returned = arrived
    returned = returned.reshape(slot_total, -1)
    seq_count = normed.shape[0]
    own_rows = lax.dynamic_slice_in_dim(
        combine_rows, lax.axis_index("replica") * seq_count, seq_count, 0
    )
    moe_out = jnp.dot(
        own_rows, returned, precision=lax.Precision.HIGHEST, preferred_element_type=jnp.float32
    )
    return (hidden_state + moe_out).astype(jnp.bfloat16)


def solution(mesh):
    in_specs = (
        P(("groups", "expert", "replica"), None),
        P(("groups", "expert", "replica"), None),
        P(("groups", "expert", "replica"), None),
        P(("groups", "expert", "replica"), None, None),
        P(("groups", "expert", "replica"), None, None),
        P(("groups", "expert", "replica")),
        P(("groups", "expert", "replica"), None),
        P(("expert", "replica"), None),
        P(),
        P(("groups", "expert"), None),
        P(("groups", "expert"), None),
        P("expert", None, "replica"),
        P("expert", None, "replica"),
        P("expert", "replica", None),
    )
    out_specs = P(("groups", "expert", "replica"), None)
    return jax.shard_map(
        on_device, mesh=mesh, in_specs=in_specs, out_specs=out_specs, check_vma=False
    )
```

profile of v0, /device:TPU:0, one launch (start us, length us, event | category | flops | bytes accessed | tf_op | source)
XLA Modules:
  0.0 200.0 jit_solution(9605539332392520658)
XLA Ops:
  6.6 4.1 %constant_dynamic-slice_fusion.15 = (bf16[256,512]{1,0:T(8,128)(2,1)}, bf16[256,512]{1,0:T(8,128)(2,1)}, bf16[256,512]{1,0:T(8,128)(2,1)}, bf16[256,512]{1,0:T(8...) fusion(bf16[256,4096]{1,0:T(8,128)(2,1)} %param.21, ...), kind=kLoop, calls=%fused_computation.59 | loop fusion | bytes 7864380 | tf_op jit(solution)/shard_map/dynamic_slice | solution.py:90
  10.7 6.0 %collective-permute-start = (bf16[256,512]{1,0:T(8,128)(2,1)}, bf16[256,512]{1,0:T(8,128)(2,1)}, u32[]{:S(2)}, u32[]{:S(2)}) collective-permute-start(bf16[256,512]{1,0:T(8,128)(2,1)} %get-tuple-element.7), channel_id=1, source_target_pairs={{0,7},{1,8},{2,9},{3,10},{4,11},{5,12},{6,13},{7,14},{8,15},{9,16}... | collective-permute-start | bytes 786440 | tf_op jit(solution)/shard_map/ppermute | solution.py:13
  16.7 4.1 %collective-permute-start.1 = (bf16[256,512]{1,0:T(8,128)(2,1)}, bf16[256,512]{1,0:T(8,128)(2,1)}, u32[]{:S(2)}, u32[]{:S(2)}) collective-permute-start(bf16[256,512]{1,0:T(8,128)(2,1)} %get-tuple-element.19), channel_id=1, source_target_pairs={{0,6},{1,7},{2,8},{3,9},{4,10},{5,11},{6,12},{7,13},{8,14},{9,15},... | collective-permute-start | bytes 786440 | tf_op jit(solution)/shard_map/ppermute | solution.py:13
  25.0 1.7 fusion.27
  27.7 1.6 fusion.8
  30.4 9.3 %all-to-all-start = ((bf16[4,32,2048]{2,0,1:T(4,128)(2,1)}), bf16[4,32,2048]{2,0,1:T(4,128)(2,1)}, u32[]{:S(2)}, u32[]{:S(2)}) async-start(bf16[4,32,2048]{2,0,1:T(4,128)(2,1)} %bitcast.67), calls=%async_computation | async-start | bytes 1048576 | tf_op jit(solution)/shard_map/all_to_all | solution.py:101
  41.1 4.0 %collective-permute-start.2 = (bf16[256,512]{1,0:T(8,128)(2,1)}, bf16[256,512]{1,0:T(8,128)(2,1)}, u32[]{:S(2)}, u32[]{:S(2)}) collective-permute-start(bf16[256,512]{1,0:T(8,128)(2,1)} %get-tuple-element.18), channel_id=1, source_target_pairs={{0,5},{1,6},{2,7},{3,8},{4,9},{5,10},{6,11},{7,12},{8,13},{9,14},{... | collective-permute-start | bytes 786440 | tf_op jit(solution)/shard_map/ppermute | solution.py:13
  45.2 6.2 %collective-permute-start.3 = (bf16[256,512]{1,0:T(8,128)(2,1)}, bf16[256,512]{1,0:T(8,128)(2,1)}, u32[]{:S(2)}, u32[]{:S(2)}) collective-permute-start(bf16[256,512]{1,0:T(8,128)(2,1)} %get-tuple-element.17), channel_id=1, source_target_pairs={{0,4},{1,5},{2,6},{3,7},{4,8},{5,9},{6,10},{7,11},{8,12},{9,13},{1... | collective-permute-start | bytes 786440 | tf_op jit(solution)/shard_map/ppermute | solution.py:13
  51.3 2.0 collective-permute-start.4
  53.6 4.2 %collective-permute-start.5 = (bf16[256,512]{1,0:T(8,128)(2,1)}, bf16[256,512]{1,0:T(8,128)(2,1)}, u32[]{:S(2)}, u32[]{:S(2)}) collective-permute-start(bf16[256,512]{1,0:T(8,128)(2,1)} %get-tuple-element.15), channel_id=1, source_target_pairs={{0,2},{1,3},{2,4},{3,5},{4,6},{5,7},{6,8},{7,9},{8,10},{9,11},{10,... | collective-permute-start | bytes 786440 | tf_op jit(solution)/shard_map/ppermute | solution.py:13
  57.9 2.0 %collective-permute-start.6 = (bf16[256,512]{1,0:T(8,128)(2,1)}, bf16[256,512]{1,0:T(8,128)(2,1)}, u32[]{:S(2)}, u32[]{:S(2)}) collective-permute-start(bf16[256,512]{1,0:T(8,128)(2,1)} %get-tuple-element.14), channel_id=1, source_target_pairs={{0,1},{1,2},{2,3},{3,4},{4,5},{5,6},{6,7},{7,8},{8,9},{9,10},{10,1... | collective-permute-start | bytes 786440 | tf_op jit(solution)/shard_map/ppermute | solution.py:13
  59.9 6.0 %collective-permute-done.2 = bf16[256,512]{1,0:T(8,128)(2,1)} collective-permute-done((bf16[256,512]{1,0:T(8,128)(2,1)}, bf16[256,512]{1,0:T(8,128)(2,1)}, u32[]{:S(2)}, u32[]{:S(2)}) %collective-permute-start.2) | collective-permute-done | bytes 262176 | tf_op jit(solution)/shard_map/ppermute | solution.py:13
  67.1 6.5 %collective-permute-done.3 = bf16[256,512]{1,0:T(8,128)(2,1)} collective-permute-done((bf16[256,512]{1,0:T(8,128)(2,1)}, bf16[256,512]{1,0:T(8,128)(2,1)}, u32[]{:S(2)}, u32[]{:S(2)}) %collective-permute-start.3) | collective-permute-done | bytes 262176 | tf_op jit(solution)/shard_map/ppermute | solution.py:13
  79.7 4.6 %collective-permute-done.8 = bf16[256,512]{1,0:T(8,128)(2,1)} collective-permute-done((bf16[256,512]{1,0:T(8,128)(2,1)}, bf16[256,512]{1,0:T(8,128)(2,1)}, u32[]{:S(2)}, u32[]{:S(2)}) %collective-permute-start.8) | collective-permute-done | bytes 262176 | tf_op jit(solution)/shard_map/ppermute | solution.py:13
  85.0 5.1 %select_select_fusion = bf16[8,256,512]{2,1,0:T(8,128)(2,1)} fusion(pred[8]{0:T(512)(128)(4,1)S(1)} %get-tuple-element.26, pred[8]{0:T(512)(128)(4,1)S(1)} %get-tuple-element.27, pred[8]{0:T(512)(128)(4,1)S(1)} %get-tuple-element.28, pred[8]{0:T(512)(128)(4,1)S(1)} %get-tuple-element.29, pred[8]{0:T(512)(128)(4,1)S(1)} %get-tuple-element.30, ...), kind=kLoop, calls=%fused_computation.9 | loop fusion | flops 15728640 | bytes 6029432 | tf_op jit(solution)/shard_map/jit(_where)/select_n | solution.py:94
  90.1 2.0 reshape.589
  92.1 2.2 %fusion.7 = bf16[128,1,512]{2,0,1:T(8,128)(2,1)S(1)} fusion(bf16[128,2048]{1,0:T(8,128)(2,1)} %reshape.589, bf16[2048,512]{1,0:T(8,128)(2,1)} %bitcast.66), kind=kOutput, calls=%fused_computation.13 | convolution fusion | flops 268500992 | bytes 2752512 | tf_op jit(solution)/shard_map/dot_general | solution.py:105
  96.3 7.8 %all-to-all-start.1 = ((bf16[32,2,1024]{2,1,0:T(2,128)(2,1)}), bf16[32,2,1024]{2,1,0:T(2,128)(2,1)S(1)}, u32[]{:S(2)}, u32[]{:S(2)}) async-start(bf16[32,2,1024]{2,1,0:T(2,128)(2,1)} %reshape.604), calls=%async_computation.1 | async-start | bytes 262144 | tf_op jit(solution)/shard_map/all_to_all | solution.py:107
  106.3 6.0 %all-to-all-done.1 = bf16[32,2,1024]{2,1,0:T(2,128)(2,1)S(1)} async-done(((bf16[32,2,1024]{2,1,0:T(2,128)(2,1)}), bf16[32,2,1024]{2,1,0:T(2,128)(2,1)S(1)}, u32[]{:S(2)}, u32[]{:S(2)}) %all-to-all-start.1) | async-done | bytes 131104 | tf_op jit(solution)/shard_map/all_to_all | solution.py:107
  114.6 1.9 all-gather
  116.5 1.8 convolution_convert_fusion.1
  118.3 2.0 %reshape.591 = bf16[16,4,4096]{2,1,0:T(4,128)(2,1)} reshape(bf16[64,4096]{1,0:T(8,128)(2,1)} %convolution_convert_fusion.1) | data formatting | bytes 1048576 | tf_op jit(solution)/shard_map/reshape | solution.py:142
  120.3 19.7 %all_to_all.34 = bf16[16,4,4096]{2,1,0:T(4,128)(2,1)} all-to-all(bf16[16,4,4096]{2,1,0:T(4,128)(2,1)} %reshape.591), channel_id=1, replica_groups=mesh['groups'=1,'expert'=16,'replica'=2] {'expert'}, dimensions={0} | all-to-all | bytes 1048576 | tf_op jit(solution)/shard_map/all_to_all | solution.py:145
  140.0 2.0 reshape.592
  142.0 2.8 %fusion.4 = f32[64,384]{1,0:T(8,128)S(1)} fusion(bf16[64,4096]{1,0:T(8,128)(2,1)} %reshape.592, bf16[1,4096,384]{2,1,0:T(8,128)(2,1)} %param.25), kind=kOutput, calls=%fused_computation.7 | convolution fusion | flops 201326592 | bytes 3768320 | tf_op jit(solution)/shard_map/dot_general | solution.py:149
  145.8 1.5 convolution_convert_fusion
  147.3 17.3 %all-reduce.2.cloned.1.call-done = bf16[16,4,4096]{2,0,1:T(8,128)(2,1)} async-done(((bf16[16,4,4096]{2,0,1:T(8,128)(2,1)}), bf16[16,4,4096]{2,0,1:T(8,128)(2,1)}) %all-reduce.2.cloned.1.call-update) | async-done | bytes 524304 | tf_op jit(solution)/shard_map/psum | solution.py:155
  164.6 2.2 %copy.34 = bf16[16,4,4096]{2,1,0:T(4,128)(2,1)} copy(bf16[16,4,4096]{2,0,1:T(8,128)(2,1)} %all-reduce.2.cloned.1.call-done) | data formatting | bytes 1048576 | tf_op jit(solution)/shard_map/psum | solution.py:155
  166.8 6.9 %all-to-all-start.3 = ((bf16[16,4,4096]{2,1,0:T(4,128)(2,1)}), bf16[16,4,4096]{2,1,0:T(4,128)(2,1)}, u32[]{:S(2)}, u32[]{:S(2)}) async-start(bf16[16,4,4096]{2,1,0:T(4,128)(2,1)} %copy.34), calls=%async_computation.3 | async-start | bytes 1048576 | tf_op jit(solution)/shard_map/all_to_all | solution.py:156
  173.7 15.5 %all-to-all-done.3 = bf16[16,4,4096]{2,1,0:T(4,128)(2,1)} async-done(((bf16[16,4,4096]{2,1,0:T(4,128)(2,1)}), bf16[16,4,4096]{2,1,0:T(4,128)(2,1)}, u32[]{:S(2)}, u32[]{:S(2)}) %all-to-all-start.3) | async-done | bytes 524320 | tf_op jit(solution)/shard_map/all_to_all | solution.py:156
  189.2 2.0 reshape.593
  191.2 2.0 fusion
  (84 shorter events, 23.3 us)
Async XLA Ops:
  6.5 139.2 %copy-start = (bf16[1,384,4096]{2,1,0:T(8,128)(2,1)S(1)}, bf16[1,384,4096]{2,1,0:T(8,128)(2,1)}, u32[]{:S(2)}) copy-start(bf16[1,384,4096]{2,1,0:T(8,128)(2,1)} %param.27) | copy-start | bytes 9437188
  6.5 18.2 %copy-start.5 = (bf16[4,8192]{1,0:T(4,128)(2,1)S(1)}, bf16[4,8192]{1,0:T(4,128)(2,1)}, u32[]{:S(2)}) copy-start(bf16[4,8192]{1,0:T(4,128)(2,1)} %param.14) | copy-start | bytes 196612
  6.5 18.2 %copy-start.10 = (s32[4]{0:T(128)S(1)}, s32[4]{0:T(128)}, u32[]{:S(2)}) copy-start(s32[4]{0:T(128)} %param.19) | copy-start | bytes 52
  6.5 18.3 %copy-start.8 = (bf16[4,512]{1,0:T(4,128)(2,1)S(1)}, bf16[4,512]{1,0:T(4,128)(2,1)}, u32[]{:S(2)}) copy-start(bf16[4,512]{1,0:T(4,128)(2,1)} %param.15) | copy-start | bytes 12292
  6.5 21.1 %copy-start.9 = (bf16[4,512]{1,0:T(4,128)(2,1)S(1)}, bf16[4,512]{1,0:T(4,128)(2,1)}, u32[]{:S(2)}) copy-start(bf16[4,512]{1,0:T(4,128)(2,1)} %param.16) | copy-start | bytes 12292
  10.7 29.1 %collective-permute-start = (bf16[256,512]{1,0:T(8,128)(2,1)}, bf16[256,512]{1,0:T(8,128)(2,1)}, u32[]{:S(2)}, u32[]{:S(2)}) collective-permute-start(bf16[256,512]{1,0:T(8,128)(2,1)} %get-tuple-element.7), channel_id=1, source_target_pairs={{0,7},{1,8},{2,9},{3,10},{4,11},{5,12},{6,13},{7,14},{8,15},{9,16}... | collective-permute-start | bytes 786440 | tf_op jit(solution)/shard_map/ppermute | solution.py:13
  16.7 24.5 %collective-permute-start.1 = (bf16[256,512]{1,0:T(8,128)(2,1)}, bf16[256,512]{1,0:T(8,128)(2,1)}, u32[]{:S(2)}, u32[]{:S(2)}) collective-permute-start(bf16[256,512]{1,0:T(8,128)(2,1)} %get-tuple-element.19), channel_id=1, source_target_pairs={{0,6},{1,7},{2,8},{3,9},{4,10},{5,11},{6,12},{7,13},{8,14},{9,15},... | collective-permute-start | bytes 786440 | tf_op jit(solution)/shard_map/ppermute | solution.py:13
  20.8 24.4 %collective-permute-start.10 = (bf16[256,512]{1,0:T(8,128)(2,1)}, bf16[256,512]{1,0:T(8,128)(2,1)}, u32[]{:S(2)}, u32[]{:S(2)}) collective-permute-start(bf16[256,512]{1,0:T(8,128)(2,1)} %get-tuple-element.10), channel_id=1, source_target_pairs={{4,0},{5,1},{6,2},{7,3},{8,4},{9,5},{10,6},{11,7},{12,8},{13,9},{1... | collective-permute-start | bytes 786440 | tf_op jit(solution)/shard_map/ppermute | solution.py:13
  22.1 29.2 %collective-permute-start.11 = (bf16[256,512]{1,0:T(8,128)(2,1)}, bf16[256,512]{1,0:T(8,128)(2,1)}, u32[]{:S(2)}, u32[]{:S(2)}) collective-permute-start(bf16[256,512]{1,0:T(8,128)(2,1)} %get-tuple-element.9), channel_id=1, source_target_pairs={{5,0},{6,1},{7,2},{8,3},{9,4},{10,5},{11,6},{12,7},{13,8},{14,9},{... | collective-permute-start | bytes 786440 | tf_op jit(solution)/shard_map/ppermute | solution.py:13
  23.4 30.2 %collective-permute-start.12 = (bf16[256,512]{1,0:T(8,128)(2,1)}, bf16[256,512]{1,0:T(8,128)(2,1)}, u32[]{:S(2)}, u32[]{:S(2)}) collective-permute-start(bf16[256,512]{1,0:T(8,128)(2,1)} %get-tuple-element.8), channel_id=1, source_target_pairs={{6,0},{7,1},{8,2},{9,3},{10,4},{11,5},{12,6},{13,7},{14,8},{15,9},... | collective-permute-start | bytes 786440 | tf_op jit(solution)/shard_map/ppermute | solution.py:13
  26.7 0.7 copy-start.3
  27.7 25.7 %copy-start.6 = (s32[8,8]{1,0:T(8,128)S(1)}, s32[8,8]{1,0:T(8,128)}, u32[]{:S(2)}) copy-start(s32[8,8]{1,0:T(8,128)} %param.23) | copy-start | bytes 772
  30.4 59.6 %all-to-all-start = ((bf16[4,32,2048]{2,0,1:T(4,128)(2,1)}), bf16[4,32,2048]{2,0,1:T(4,128)(2,1)}, u32[]{:S(2)}, u32[]{:S(2)}) async-start(bf16[4,32,2048]{2,0,1:T(4,128)(2,1)} %bitcast.67), calls=%async_computation | async-start | bytes 1048576 | tf_op jit(solution)/shard_map/all_to_all | solution.py:101
  39.8 18.0 %collective-permute-start.13 = (bf16[256,512]{1,0:T(8,128)(2,1)}, bf16[256,512]{1,0:T(8,128)(2,1)}, u32[]{:S(2)}, u32[]{:S(2)}) collective-permute-start(bf16[256,512]{1,0:T(8,128)(2,1)} %get-tuple-element.21), channel_id=1, source_target_pairs={{7,0},{8,1},{9,2},{10,3},{11,4},{12,5},{13,6},{14,7},{15,8},{16,9}... | collective-permute-start | bytes 786440 | tf_op jit(solution)/shard_map/ppermute | solution.py:13
  41.1 24.7 %collective-permute-start.2 = (bf16[256,512]{1,0:T(8,128)(2,1)}, bf16[256,512]{1,0:T(8,128)(2,1)}, u32[]{:S(2)}, u32[]{:S(2)}) collective-permute-start(bf16[256,512]{1,0:T(8,128)(2,1)} %get-tuple-element.18), channel_id=1, source_target_pairs={{0,5},{1,6},{2,7},{3,8},{4,9},{5,10},{6,11},{7,12},{8,13},{9,14},{... | collective-permute-start | bytes 786440 | tf_op jit(solution)/shard_map/ppermute | solution.py:13
  45.2 28.4 %collective-permute-start.3 = (bf16[256,512]{1,0:T(8,128)(2,1)}, bf16[256,512]{1,0:T(8,128)(2,1)}, u32[]{:S(2)}, u32[]{:S(2)}) collective-permute-start(bf16[256,512]{1,0:T(8,128)(2,1)} %get-tuple-element.17), channel_id=1, source_target_pairs={{0,4},{1,5},{2,6},{3,7},{4,8},{5,9},{6,10},{7,11},{8,12},{9,13},{1... | collective-permute-start | bytes 786440 | tf_op jit(solution)/shard_map/ppermute | solution.py:13
  51.3 23.6 %collective-permute-start.4 = (bf16[256,512]{1,0:T(8,128)(2,1)}, bf16[256,512]{1,0:T(8,128)(2,1)}, u32[]{:S(2)}, u32[]{:S(2)}) collective-permute-start(bf16[256,512]{1,0:T(8,128)(2,1)} %get-tuple-element.16), channel_id=1, source_target_pairs={{0,3},{1,4},{2,5},{3,6},{4,7},{5,8},{6,9},{7,10},{8,11},{9,12},{10... | collective-permute-start | bytes 786440 | tf_op jit(solution)/shard_map/ppermute | solution.py:13
  53.6 26.0 %collective-permute-start.5 = (bf16[256,512]{1,0:T(8,128)(2,1)}, bf16[256,512]{1,0:T(8,128)(2,1)}, u32[]{:S(2)}, u32[]{:S(2)}) collective-permute-start(bf16[256,512]{1,0:T(8,128)(2,1)} %get-tuple-element.15), channel_id=1, source_target_pairs={{0,2},{1,3},{2,4},{3,5},{4,6},{5,7},{6,8},{7,9},{8,10},{9,11},{10,... | collective-permute-start | bytes 786440 | tf_op jit(solution)/shard_map/ppermute | solution.py:13
  57.9 21.8 %collective-permute-start.6 = (bf16[256,512]{1,0:T(8,128)(2,1)}, bf16[256,512]{1,0:T(8,128)(2,1)}, u32[]{:S(2)}, u32[]{:S(2)}) collective-permute-start(bf16[256,512]{1,0:T(8,128)(2,1)} %get-tuple-element.14), channel_id=1, source_target_pairs={{0,1},{1,2},{2,3},{3,4},{4,5},{5,6},{6,7},{7,8},{8,9},{9,10},{10,1... | collective-permute-start | bytes 786440 | tf_op jit(solution)/shard_map/ppermute | solution.py:13
  65.9 13.8 %collective-permute-start.7 = (bf16[256,512]{1,0:T(8,128)(2,1)}, bf16[256,512]{1,0:T(8,128)(2,1)}, u32[]{:S(2)}, u32[]{:S(2)}) collective-permute-start(bf16[256,512]{1,0:T(8,128)(2,1)} %get-tuple-element.13), channel_id=1, source_target_pairs={{1,0},{2,1},{3,2},{4,3},{5,4},{6,5},{7,6},{8,7},{9,8},{10,9},{11,1... | collective-permute-start | bytes 786440 | tf_op jit(solution)/shard_map/ppermute | solution.py:13
  73.6 10.6 %collective-permute-start.8 = (bf16[256,512]{1,0:T(8,128)(2,1)}, bf16[256,512]{1,0:T(8,128)(2,1)}, u32[]{:S(2)}, u32[]{:S(2)}) collective-permute-start(bf16[256,512]{1,0:T(8,128)(2,1)} %get-tuple-element.12), channel_id=1, source_target_pairs={{2,0},{3,1},{4,2},{5,3},{6,4},{7,5},{8,6},{9,7},{10,8},{11,9},{12,... | collective-permute-start | bytes 786440 | tf_op jit(solution)/shard_map/ppermute | solution.py:13
  74.9 10.1 %collective-permute-start.9 = (bf16[256,512]{1,0:T(8,128)(2,1)}, bf16[256,512]{1,0:T(8,128)(2,1)}, u32[]{:S(2)}, u32[]{:S(2)}) collective-permute-start(bf16[256,512]{1,0:T(8,128)(2,1)} %get-tuple-element.11), channel_id=1, source_target_pairs={{3,0},{4,1},{5,2},{6,3},{7,4},{8,5},{9,6},{10,7},{11,8},{12,9},{13... | collective-permute-start | bytes 786440 | tf_op jit(solution)/shard_map/ppermute | solution.py:13
  96.3 16.1 %all-to-all-start.1 = ((bf16[32,2,1024]{2,1,0:T(2,128)(2,1)}), bf16[32,2,1024]{2,1,0:T(2,128)(2,1)S(1)}, u32[]{:S(2)}, u32[]{:S(2)}) async-start(bf16[32,2,1024]{2,1,0:T(2,128)(2,1)} %reshape.604), calls=%async_computation.1 | async-start | bytes 262144 | tf_op jit(solution)/shard_map/all_to_all | solution.py:107
  104.1 60.5 %all-reduce.2.cloned.1.call-start = ((), (), s32[]{:S(2)}) async-start(), calls=%async_computation.4 | async-start | bytes 1048576 | tf_op jit(solution)/shard_map/psum | solution.py:155
  142.0 2.8 %copy-start.1 = (bf16[64,4096]{1,0:T(8,128)(2,1)S(1)}, bf16[64,4096]{1,0:T(8,128)(2,1)}, u32[]{:S(2)}) copy-start(bf16[64,4096]{1,0:T(8,128)(2,1)} %reshape.592) | copy-start | bytes 1572868
  142.0 3.2 %copy-start.2 = (bf16[1,4096,384]{2,1,0:T(8,128)(2,1)S(1)}, bf16[1,4096,384]{2,1,0:T(8,128)(2,1)}, u32[]{:S(2)}) copy-start(bf16[1,4096,384]{2,1,0:T(8,128)(2,1)} %param.26) | copy-start | bytes 9437188
  147.2 44.0 %copy-start.4 = (bf16[4,4096]{1,0:T(4,128)(2,1)S(1)}, bf16[4,4096]{1,0:T(4,128)(2,1)}, u32[]{:S(2)}) copy-start(bf16[4,4096]{1,0:T(4,128)(2,1)} %param.20) | copy-start | bytes 98308
  147.2 44.0 %copy-start.7 = (f32[64,8]{0,1:T(8,128)S(1)}, f32[64,8]{0,1:T(8,128)}, u32[]{:S(2)}) copy-start(f32[64,8]{0,1:T(8,128)} %get-tuple-element.5) | copy-start | bytes 6148
  166.8 22.4 %all-to-all-start.3 = ((bf16[16,4,4096]{2,1,0:T(4,128)(2,1)}), bf16[16,4,4096]{2,1,0:T(4,128)(2,1)}, u32[]{:S(2)}, u32[]{:S(2)}) async-start(bf16[16,4,4096]{2,1,0:T(4,128)(2,1)} %copy.34), calls=%async_computation.3 | async-start | bytes 1048576 | tf_op jit(solution)/shard_map/all_to_all | solution.py:156
Sparse Core Ops, SparseCore 0:
  147.4 17.1 all-reduce.1
where the time goes:
time: 202 us; the launch traced here: 200 us
  starting transfers between devices  61.6 us (30%)
  waiting for transfers between devices  56.7 us (28%)
  blocking collectives  21.6 us (11%)
  local copies, waits for them, and re-layouts  18.3 us (9%)
  matrix products  14.3 us (7%)
  other arithmetic  13.8 us (7%)
  between operations  13.8 us (7%)
    ppermute x14, starting transfers between devices, shifted(): return lax.ppermute(block, axis, route)  37.6 us
    all_to_all x1, blocking collectives, on_device(): lax.all_to_all(outgoing, 'expert', split_axis=0, concat_axis=0, tiled=True)  19.7 us
    ppermute x14, waiting for transfers between devices, shifted(): return lax.ppermute(block, axis, route)  17.8 us
    psum x1, waiting for transfers between devices, on_device(): lax.psum(partial_value.astype(jnp.bfloat16), 'replica').astype(jnp.float32)  17.3 us
    all_to_all x1, waiting for transfers between devices, on_device(): lax.all_to_all(summed_halves.astype(jnp.bfloat16), 'expert', split_axis=0...  15.5 us
    all_to_all x1, starting transfers between devices, on_device(): lax.all_to_all(repeated, ('expert', 'replica'), split_axis=1, concat_axis...  9.28 us
    all_to_all x1, starting transfers between devices, on_device(): lax.all_to_all(partial_cols.astype(jnp.bfloat16), ('expert', 'replica'),...  7.84 us
    all_to_all x1, starting transfers between devices, on_device(): lax.all_to_all(summed_halves.astype(jnp.bfloat16), 'expert', split_axis=0...  6.88 us
  transfers between devices with their start and end apart: 18, of which 7 were waited for; matrix products, arithmetic and copies ran while one was open for 8% of the time, Pallas kernels for 0%

commit v1 on v0

--- a/solution.py
+++ b/solution.py
@@ -152,7 +152,9 @@
     partial_value = jnp.dot(hidden_act, w_down[0], preferred_element_type=jnp.float32).reshape(
         lead_shape + (model_width,)
     )
-    summed_halves = lax.psum(partial_value.astype(jnp.bfloat16), "replica").astype(jnp.float32)
+    summed_halves = jnp.sum(
+        lax.all_gather(partial_value.astype(jnp.bfloat16), "replica"), axis=0
+    ).astype(jnp.float32)
     arrived = lax.all_to_all(
         summed_halves.astype(jnp.bfloat16), "expert", split_axis=0, concat_axis=0, tiled=True
     ).astype(summed_halves.dtype)

time: 202 us -> 194 us (0.960)
  waiting for transfers between devices: 56.7 us -> 47.1 us
  other arithmetic: 13.8 us -> 16.2 us
    psum x1 -> x0, waiting for transfers between devices: 17.3 us -> none  [on_device(): lax.psum(partial_value.astype(jnp.bfloat16), 'replica').astype(jnp.float32)]
    all_gather x0 -> x1, waiting for transfers between devices: none -> 7.72 us  [on_device(): lax.all_gather(partial_value.astype(jnp.bfloat16), 'replica')]
    reduce_sum x0 -> x1, other arithmetic: none -> 2.37 us  [on_device(): jnp.sum(lax.all_gather(partial_value.astype(jnp.bfloat16), 'replica'), ax...]
    psum x1 -> x0, local copies, waits for them, and re-layouts: 2.25 us -> none  [on_device(): lax.psum(partial_value.astype(jnp.bfloat16), 'replica').astype(jnp.float32)]
    reduce_sum x0 -> x1, local copies, waits for them, and re-layouts: none -> 2.25 us  [on_device(): jnp.sum(lax.all_gather(partial_value.astype(jnp.bfloat16), 'replica'), ax...]
where the time goes in v1:
time: 194 us; the launch traced here: 193 us
  starting transfers between devices  61.6 us (32%)
  waiting for transfers between devices  47.1 us (24%)
  blocking collectives  21.6 us (11%)
  local copies, waits for them, and re-layouts  18.3 us (9%)
  other arithmetic  16.2 us (8%)
  matrix products  14.3 us (7%)
  between operations  13.8 us (7%)
    ppermute x14, starting transfers between devices, shifted(): return lax.ppermute(block, axis, route)  37.6 us
    all_to_all x1, blocking collectives, on_device(): lax.all_to_all(outgoing, 'expert', split_axis=0, concat_axis=0, tiled=True)  19.7 us
    ppermute x14, waiting for transfers between devices, shifted(): return lax.ppermute(block, axis, route)  17.8 us
    all_to_all x1, waiting for transfers between devices, on_device(): lax.all_to_all(summed_halves.astype(jnp.bfloat16), 'expert', split_axis=0...  15.5 us
    all_to_all x1, starting transfers between devices, on_device(): lax.all_to_all(repeated, ('expert', 'replica'), split_axis=1, concat_axis...  9.28 us
    all_to_all x1, starting transfers between devices, on_device(): lax.all_to_all(partial_cols.astype(jnp.bfloat16), ('expert', 'replica'),...  7.84 us
    all_gather x1, waiting for transfers between devices, on_device(): lax.all_gather(partial_value.astype(jnp.bfloat16), 'replica')  7.72 us
    all_to_all x1, starting transfers between devices, on_device(): lax.all_to_all(summed_halves.astype(jnp.bfloat16), 'expert', split_axis=0...  6.84 us
  transfers between devices with their start and end apart: 18, of which 7 were waited for; matrix products, arithmetic and copies ran while one was open for 8% of the time, Pallas kernels for 0%

profile of v1, /device:TPU:0, one launch (start us, length us, event | category | flops | bytes accessed | tf_op | source)
XLA Modules:
  0.0 192.8 jit_solution(16555486169572360408)
XLA Ops:
  6.6 4.1 %constant_dynamic-slice_fusion.15 = (bf16[256,512]{1,0:T(8,128)(2,1)}, bf16[256,512]{1,0:T(8,128)(2,1)}, bf16[256,512]{1,0:T(8,128)(2,1)}, bf16[256,512]{1,0:T(8...) fusion(bf16[256,4096]{1,0:T(8,128)(2,1)} %param.21, ...), kind=kLoop, calls=%fused_computation.59 | loop fusion | bytes 7864380 | tf_op jit(solution)/shard_map/dynamic_slice | solution.py:90
  10.7 6.0 %collective-permute-start = (bf16[256,512]{1,0:T(8,128)(2,1)}, bf16[256,512]{1,0:T(8,128)(2,1)}, u32[]{:S(2)}, u32[]{:S(2)}) collective-permute-start(bf16[256,512]{1,0:T(8,128)(2,1)} %get-tuple-element.7), channel_id=1, source_target_pairs={{0,7},{1,8},{2,9},{3,10},{4,11},{5,12},{6,13},{7,14},{8,15},{9,16}... | collective-permute-start | bytes 786440 | tf_op jit(solution)/shard_map/ppermute | solution.py:13
  16.7 4.1 %collective-permute-start.1 = (bf16[256,512]{1,0:T(8,128)(2,1)}, bf16[256,512]{1,0:T(8,128)(2,1)}, u32[]{:S(2)}, u32[]{:S(2)}) collective-permute-start(bf16[256,512]{1,0:T(8,128)(2,1)} %get-tuple-element.19), channel_id=1, source_target_pairs={{0,6},{1,7},{2,8},{3,9},{4,10},{5,11},{6,12},{7,13},{8,14},{9,15},... | collective-permute-start | bytes 786440 | tf_op jit(solution)/shard_map/ppermute | solution.py:13
  25.0 1.7 fusion.27
  27.7 1.6 fusion.8
  30.4 9.3 %all-to-all-start = ((bf16[4,32,2048]{2,0,1:T(4,128)(2,1)}), bf16[4,32,2048]{2,0,1:T(4,128)(2,1)}, u32[]{:S(2)}, u32[]{:S(2)}) async-start(bf16[4,32,2048]{2,0,1:T(4,128)(2,1)} %bitcast.68), calls=%async_computation | async-start | bytes 1048576 | tf_op jit(solution)/shard_map/all_to_all | solution.py:101
  41.1 4.0 %collective-permute-start.2 = (bf16[256,512]{1,0:T(8,128)(2,1)}, bf16[256,512]{1,0:T(8,128)(2,1)}, u32[]{:S(2)}, u32[]{:S(2)}) collective-permute-start(bf16[256,512]{1,0:T(8,128)(2,1)} %get-tuple-element.18), channel_id=1, source_target_pairs={{0,5},{1,6},{2,7},{3,8},{4,9},{5,10},{6,11},{7,12},{8,13},{9,14},{... | collective-permute-start | bytes 786440 | tf_op jit(solution)/shard_map/ppermute | solution.py:13
  45.2 6.2 %collective-permute-start.3 = (bf16[256,512]{1,0:T(8,128)(2,1)}, bf16[256,512]{1,0:T(8,128)(2,1)}, u32[]{:S(2)}, u32[]{:S(2)}) collective-permute-start(bf16[256,512]{1,0:T(8,128)(2,1)} %get-tuple-element.17), channel_id=1, source_target_pairs={{0,4},{1,5},{2,6},{3,7},{4,8},{5,9},{6,10},{7,11},{8,12},{9,13},{1... | collective-permute-start | bytes 786440 | tf_op jit(solution)/shard_map/ppermute | solution.py:13
  51.3 2.0 %collective-permute-start.4 = (bf16[256,512]{1,0:T(8,128)(2,1)}, bf16[256,512]{1,0:T(8,128)(2,1)}, u32[]{:S(2)}, u32[]{:S(2)}) collective-permute-start(bf16[256,512]{1,0:T(8,128)(2,1)} %get-tuple-element.16), channel_id=1, source_target_pairs={{0,3},{1,4},{2,5},{3,6},{4,7},{5,8},{6,9},{7,10},{8,11},{9,12},{10... | collective-permute-start | bytes 786440 | tf_op jit(solution)/shard_map/ppermute | solution.py:13
  53.6 4.2 %collective-permute-start.5 = (bf16[256,512]{1,0:T(8,128)(2,1)}, bf16[256,512]{1,0:T(8,128)(2,1)}, u32[]{:S(2)}, u32[]{:S(2)}) collective-permute-start(bf16[256,512]{1,0:T(8,128)(2,1)} %get-tuple-element.15), channel_id=1, source_target_pairs={{0,2},{1,3},{2,4},{3,5},{4,6},{5,7},{6,8},{7,9},{8,10},{9,11},{10,... | collective-permute-start | bytes 786440 | tf_op jit(solution)/shard_map/ppermute | solution.py:13
  57.9 2.0 %collective-permute-start.6 = (bf16[256,512]{1,0:T(8,128)(2,1)}, bf16[256,512]{1,0:T(8,128)(2,1)}, u32[]{:S(2)}, u32[]{:S(2)}) collective-permute-start(bf16[256,512]{1,0:T(8,128)(2,1)} %get-tuple-element.14), channel_id=1, source_target_pairs={{0,1},{1,2},{2,3},{3,4},{4,5},{5,6},{6,7},{7,8},{8,9},{9,10},{10,1... | collective-permute-start | bytes 786440 | tf_op jit(solution)/shard_map/ppermute | solution.py:13
  59.9 6.0 %collective-permute-done.2 = bf16[256,512]{1,0:T(8,128)(2,1)} collective-permute-done((bf16[256,512]{1,0:T(8,128)(2,1)}, bf16[256,512]{1,0:T(8,128)(2,1)}, u32[]{:S(2)}, u32[]{:S(2)}) %collective-permute-start.2) | collective-permute-done | bytes 262176 | tf_op jit(solution)/shard_map/ppermute | solution.py:13
  67.1 6.5 %collective-permute-done.3 = bf16[256,512]{1,0:T(8,128)(2,1)} collective-permute-done((bf16[256,512]{1,0:T(8,128)(2,1)}, bf16[256,512]{1,0:T(8,128)(2,1)}, u32[]{:S(2)}, u32[]{:S(2)}) %collective-permute-start.3) | collective-permute-done | bytes 262176 | tf_op jit(solution)/shard_map/ppermute | solution.py:13
  79.7 4.6 %collective-permute-done.8 = bf16[256,512]{1,0:T(8,128)(2,1)} collective-permute-done((bf16[256,512]{1,0:T(8,128)(2,1)}, bf16[256,512]{1,0:T(8,128)(2,1)}, u32[]{:S(2)}, u32[]{:S(2)}) %collective-permute-start.8) | collective-permute-done | bytes 262176 | tf_op jit(solution)/shard_map/ppermute | solution.py:13
  85.0 5.1 %select_select_fusion = bf16[8,256,512]{2,1,0:T(8,128)(2,1)} fusion(pred[8]{0:T(512)(128)(4,1)S(1)} %get-tuple-element.26, pred[8]{0:T(512)(128)(4,1)S(1)} %get-tuple-element.27, pred[8]{0:T(512)(128)(4,1)S(1)} %get-tuple-element.28, pred[8]{0:T(512)(128)(4,1)S(1)} %get-tuple-element.29, pred[8]{0:T(512)(128)(4,1)S(1)} %get-tuple-element.30, ...), kind=kLoop, calls=%fused_computation.9 | loop fusion | flops 15728640 | bytes 6029432 | tf_op jit(solution)/shard_map/jit(_where)/select_n | solution.py:94
  90.1 2.0 %reshape.589 = bf16[128,2048]{1,0:T(8,128)(2,1)} reshape(bf16[32,4,1,2048]{3,1,0,2:T(4,128)(2,1)} %bitcast.4) | data formatting | bytes 1048576 | tf_op jit(solution)/shard_map/reshape | solution.py:104
  92.1 2.2 %fusion.7 = bf16[128,1,512]{2,0,1:T(8,128)(2,1)S(1)} fusion(bf16[128,2048]{1,0:T(8,128)(2,1)} %reshape.589, bf16[2048,512]{1,0:T(8,128)(2,1)} %bitcast.67), kind=kOutput, calls=%fused_computation.13 | convolution fusion | flops 268500992 | bytes 2752512 | tf_op jit(solution)/shard_map/dot_general | solution.py:105
  96.3 7.8 %all-to-all-start.1 = ((bf16[32,2,1024]{2,1,0:T(2,128)(2,1)}), bf16[32,2,1024]{2,1,0:T(2,128)(2,1)S(1)}, u32[]{:S(2)}, u32[]{:S(2)}) async-start(bf16[32,2,1024]{2,1,0:T(2,128)(2,1)} %reshape.605), calls=%async_computation.1 | async-start | bytes 262144 | tf_op jit(solution)/shard_map/all_to_all | solution.py:107
  106.3 6.0 %all-to-all-done.1 = bf16[32,2,1024]{2,1,0:T(2,128)(2,1)S(1)} async-done(((bf16[32,2,1024]{2,1,0:T(2,128)(2,1)}), bf16[32,2,1024]{2,1,0:T(2,128)(2,1)S(1)}, u32[]{:S(2)}, u32[]{:S(2)}) %all-to-all-start.1) | async-done | bytes 131104 | tf_op jit(solution)/shard_map/all_to_all | solution.py:107
  114.6 1.9 all-gather.1
  116.5 1.8 convolution_convert_fusion.1
  118.3 2.0 %reshape.591 = bf16[16,4,4096]{2,1,0:T(4,128)(2,1)} reshape(bf16[64,4096]{1,0:T(8,128)(2,1)} %convolution_convert_fusion.1) | data formatting | bytes 1048576 | tf_op jit(solution)/shard_map/reshape | solution.py:142
  120.3 19.7 %all_to_all.34 = bf16[16,4,4096]{2,1,0:T(4,128)(2,1)} all-to-all(bf16[16,4,4096]{2,1,0:T(4,128)(2,1)} %reshape.591), channel_id=1, replica_groups=mesh['groups'=1,'expert'=16,'replica'=2] {'expert'}, dimensions={0} | all-to-all | bytes 1048576 | tf_op jit(solution)/shard_map/all_to_all | solution.py:145
  140.0 2.0 %reshape.592 = bf16[64,4096]{1,0:T(8,128)(2,1)} reshape(bf16[16,4,4096]{2,1,0:T(4,128)(2,1)} %all_to_all.34) | data formatting | bytes 1048576 | tf_op jit(solution)/shard_map/reshape | solution.py:148
  142.0 2.8 %fusion.4 = f32[64,384]{1,0:T(8,128)S(1)} fusion(bf16[64,4096]{1,0:T(8,128)(2,1)} %reshape.592, bf16[1,4096,384]{2,1,0:T(8,128)(2,1)} %param.25), kind=kOutput, calls=%fused_computation.7 | convolution fusion | flops 201326592 | bytes 3768320 | tf_op jit(solution)/shard_map/dot_general | solution.py:149
  147.3 7.7 %all-gather.4.cloned.1.call-done = bf16[32,4,4096]{2,0,1:T(8,128)(2,1)} async-done(((bf16[16,4,4096]{2,0,1:T(8,128)(2,1)}), bf16[32,4,4096]{2,0,1:T(8,128)(2,1)}) %all-gather.4.cloned.1.call-update) | async-done | bytes 1048592 | tf_op jit(solution)/shard_map/all_gather | solution.py:156
  155.0 2.4 %reduce_sum.85 = bf16[16,4,4096]{2,0,1:T(8,128)(2,1)} reduce(bf16[2,16,4,4096]{3,1,0,2:T(8,128)(2,1)} %bitcast.73, bf16[]{:T(256)} %constant.138.clone.1), dimensions={0}, to_apply=%region_8.9 | reduce | flops 262144 | bytes 1572866 | tf_op jit(solution)/shard_map/reduce_sum | solution.py:155
  157.4 2.2 %copy.44 = bf16[16,4,4096]{2,1,0:T(4,128)(2,1)} copy(bf16[16,4,4096]{2,0,1:T(8,128)(2,1)} %reduce_sum.85) | data formatting | bytes 1048576 | tf_op jit(solution)/shard_map/reduce_sum | solution.py:155
  159.6 6.8 %all-to-all-start.3 = ((bf16[16,4,4096]{2,1,0:T(4,128)(2,1)}), bf16[16,4,4096]{2,1,0:T(4,128)(2,1)}, u32[]{:S(2)}, u32[]{:S(2)}) async-start(bf16[16,4,4096]{2,1,0:T(4,128)(2,1)} %copy.44), calls=%async_computation.3 | async-start | bytes 1048576 | tf_op jit(solution)/shard_map/all_to_all | solution.py:158
  166.5 15.5 %all-to-all-done.3 = bf16[16,4,4096]{2,1,0:T(4,128)(2,1)} async-done(((bf16[16,4,4096]{2,1,0:T(4,128)(2,1)}), bf16[16,4,4096]{2,1,0:T(4,128)(2,1)}, u32[]{:S(2)}, u32[]{:S(2)}) %all-to-all-start.3) | async-done | bytes 524320 | tf_op jit(solution)/shard_map/all_to_all | solution.py:158
  182.0 2.0 %reshape.593 = bf16[64,4096]{1,0:T(8,128)(2,1)} reshape(bf16[16,4,4096]{2,1,0:T(4,128)(2,1)} %all-to-all-done.3) | data formatting | bytes 1048576 | tf_op jit(solution)/shard_map/reshape | solution.py:162
  184.0 2.0 %fusion = bf16[4,4096]{1,0:T(4,128)(2,1)} fusion(bf16[64,4096]{1,0:T(8,128)(2,1)} %reshape.593, f32[4,4096]{1,0:T(4,128)S(1)} %bitcast.71, bf16[4,4096]{1,0:T(4,128)(2,1)S(1)} %copy-done.4, f32[64,8]{0,1:T(8,128)S(1)} %copy-done.7, s32[]{:T(128)S(6)} %select_n.340), kind=kOutput, calls=%fused_computation.3 | convolution fusion | flops 12648448 | bytes 657412 | tf_op jit(solution)/shard_map/dot_general | solution.py:167
  (85 shorter events, 24.8 us)
Async XLA Ops:
  6.5 139.2 %copy-start = (bf16[1,384,4096]{2,1,0:T(8,128)(2,1)S(1)}, bf16[1,384,4096]{2,1,0:T(8,128)(2,1)}, u32[]{:S(2)}) copy-start(bf16[1,384,4096]{2,1,0:T(8,128)(2,1)} %param.27) | copy-start | bytes 9437188
  6.5 18.2 %copy-start.5 = (bf16[4,8192]{1,0:T(4,128)(2,1)S(1)}, bf16[4,8192]{1,0:T(4,128)(2,1)}, u32[]{:S(2)}) copy-start(bf16[4,8192]{1,0:T(4,128)(2,1)} %param.14) | copy-start | bytes 196612
  6.5 18.2 %copy-start.10 = (s32[4]{0:T(128)S(1)}, s32[4]{0:T(128)}, u32[]{:S(2)}) copy-start(s32[4]{0:T(128)} %param.19) | copy-start | bytes 52
  6.5 18.3 %copy-start.8 = (bf16[4,512]{1,0:T(4,128)(2,1)S(1)}, bf16[4,512]{1,0:T(4,128)(2,1)}, u32[]{:S(2)}) copy-start(bf16[4,512]{1,0:T(4,128)(2,1)} %param.15) | copy-start | bytes 12292
  6.5 21.1 %copy-start.9 = (bf16[4,512]{1,0:T(4,128)(2,1)S(1)}, bf16[4,512]{1,0:T(4,128)(2,1)}, u32[]{:S(2)}) copy-start(bf16[4,512]{1,0:T(4,128)(2,1)} %param.16) | copy-start | bytes 12292
  10.7 29.1 %collective-permute-start = (bf16[256,512]{1,0:T(8,128)(2,1)}, bf16[256,512]{1,0:T(8,128)(2,1)}, u32[]{:S(2)}, u32[]{:S(2)}) collective-permute-start(bf16[256,512]{1,0:T(8,128)(2,1)} %get-tuple-element.7), channel_id=1, source_target_pairs={{0,7},{1,8},{2,9},{3,10},{4,11},{5,12},{6,13},{7,14},{8,15},{9,16}... | collective-permute-start | bytes 786440 | tf_op jit(solution)/shard_map/ppermute | solution.py:13
  16.7 24.5 %collective-permute-start.1 = (bf16[256,512]{1,0:T(8,128)(2,1)}, bf16[256,512]{1,0:T(8,128)(2,1)}, u32[]{:S(2)}, u32[]{:S(2)}) collective-permute-start(bf16[256,512]{1,0:T(8,128)(2,1)} %get-tuple-element.19), channel_id=1, source_target_pairs={{0,6},{1,7},{2,8},{3,9},{4,10},{5,11},{6,12},{7,13},{8,14},{9,15},... | collective-permute-start | bytes 786440 | tf_op jit(solution)/shard_map/ppermute | solution.py:13
  20.8 24.4 %collective-permute-start.10 = (bf16[256,512]{1,0:T(8,128)(2,1)}, bf16[256,512]{1,0:T(8,128)(2,1)}, u32[]{:S(2)}, u32[]{:S(2)}) collective-permute-start(bf16[256,512]{1,0:T(8,128)(2,1)} %get-tuple-element.10), channel_id=1, source_target_pairs={{4,0},{5,1},{6,2},{7,3},{8,4},{9,5},{10,6},{11,7},{12,8},{13,9},{1... | collective-permute-start | bytes 786440 | tf_op jit(solution)/shard_map/ppermute | solution.py:13
  22.1 29.2 %collective-permute-start.11 = (bf16[256,512]{1,0:T(8,128)(2,1)}, bf16[256,512]{1,0:T(8,128)(2,1)}, u32[]{:S(2)}, u32[]{:S(2)}) collective-permute-start(bf16[256,512]{1,0:T(8,128)(2,1)} %get-tuple-element.9), channel_id=1, source_target_pairs={{5,0},{6,1},{7,2},{8,3},{9,4},{10,5},{11,6},{12,7},{13,8},{14,9},{... | collective-permute-start | bytes 786440 | tf_op jit(solution)/shard_map/ppermute | solution.py:13
  23.4 30.2 %collective-permute-start.12 = (bf16[256,512]{1,0:T(8,128)(2,1)}, bf16[256,512]{1,0:T(8,128)(2,1)}, u32[]{:S(2)}, u32[]{:S(2)}) collective-permute-start(bf16[256,512]{1,0:T(8,128)(2,1)} %get-tuple-element.8), channel_id=1, source_target_pairs={{6,0},{7,1},{8,2},{9,3},{10,4},{11,5},{12,6},{13,7},{14,8},{15,9},... | collective-permute-start | bytes 786440 | tf_op jit(solution)/shard_map/ppermute | solution.py:13
  26.7 0.7 copy-start.3
  27.7 25.7 %copy-start.6 = (s32[8,8]{1,0:T(8,128)S(1)}, s32[8,8]{1,0:T(8,128)}, u32[]{:S(2)}) copy-start(s32[8,8]{1,0:T(8,128)} %param.23) | copy-start | bytes 772
  30.4 59.6 %all-to-all-start = ((bf16[4,32,2048]{2,0,1:T(4,128)(2,1)}), bf16[4,32,2048]{2,0,1:T(4,128)(2,1)}, u32[]{:S(2)}, u32[]{:S(2)}) async-start(bf16[4,32,2048]{2,0,1:T(4,128)(2,1)} %bitcast.68), calls=%async_computation | async-start | bytes 1048576 | tf_op jit(solution)/shard_map/all_to_all | solution.py:101
  39.8 18.0 %collective-permute-start.13 = (bf16[256,512]{1,0:T(8,128)(2,1)}, bf16[256,512]{1,0:T(8,128)(2,1)}, u32[]{:S(2)}, u32[]{:S(2)}) collective-permute-start(bf16[256,512]{1,0:T(8,128)(2,1)} %get-tuple-element.21), channel_id=1, source_target_pairs={{7,0},{8,1},{9,2},{10,3},{11,4},{12,5},{13,6},{14,7},{15,8},{16,9}... | collective-permute-start | bytes 786440 | tf_op jit(solution)/shard_map/ppermute | solution.py:13
  41.1 24.7 %collective-permute-start.2 = (bf16[256,512]{1,0:T(8,128)(2,1)}, bf16[256,512]{1,0:T(8,128)(2,1)}, u32[]{:S(2)}, u32[]{:S(2)}) collective-permute-start(bf16[256,512]{1,0:T(8,128)(2,1)} %get-tuple-element.18), channel_id=1, source_target_pairs={{0,5},{1,6},{2,7},{3,8},{4,9},{5,10},{6,11},{7,12},{8,13},{9,14},{... | collective-permute-start | bytes 786440 | tf_op jit(solution)/shard_map/ppermute | solution.py:13
  45.2 28.4 %collective-permute-start.3 = (bf16[256,512]{1,0:T(8,128)(2,1)}, bf16[256,512]{1,0:T(8,128)(2,1)}, u32[]{:S(2)}, u32[]{:S(2)}) collective-permute-start(bf16[256,512]{1,0:T(8,128)(2,1)} %get-tuple-element.17), channel_id=1, source_target_pairs={{0,4},{1,5},{2,6},{3,7},{4,8},{5,9},{6,10},{7,11},{8,12},{9,13},{1... | collective-permute-start | bytes 786440 | tf_op jit(solution)/shard_map/ppermute | solution.py:13
  51.3 23.6 %collective-permute-start.4 = (bf16[256,512]{1,0:T(8,128)(2,1)}, bf16[256,512]{1,0:T(8,128)(2,1)}, u32[]{:S(2)}, u32[]{:S(2)}) collective-permute-start(bf16[256,512]{1,0:T(8,128)(2,1)} %get-tuple-element.16), channel_id=1, source_target_pairs={{0,3},{1,4},{2,5},{3,6},{4,7},{5,8},{6,9},{7,10},{8,11},{9,12},{10... | collective-permute-start | bytes 786440 | tf_op jit(solution)/shard_map/ppermute | solution.py:13
  53.6 26.0 %collective-permute-start.5 = (bf16[256,512]{1,0:T(8,128)(2,1)}, bf16[256,512]{1,0:T(8,128)(2,1)}, u32[]{:S(2)}, u32[]{:S(2)}) collective-permute-start(bf16[256,512]{1,0:T(8,128)(2,1)} %get-tuple-element.15), channel_id=1, source_target_pairs={{0,2},{1,3},{2,4},{3,5},{4,6},{5,7},{6,8},{7,9},{8,10},{9,11},{10,... | collective-permute-start | bytes 786440 | tf_op jit(solution)/shard_map/ppermute | solution.py:13
  57.9 21.8 %collective-permute-start.6 = (bf16[256,512]{1,0:T(8,128)(2,1)}, bf16[256,512]{1,0:T(8,128)(2,1)}, u32[]{:S(2)}, u32[]{:S(2)}) collective-permute-start(bf16[256,512]{1,0:T(8,128)(2,1)} %get-tuple-element.14), channel_id=1, source_target_pairs={{0,1},{1,2},{2,3},{3,4},{4,5},{5,6},{6,7},{7,8},{8,9},{9,10},{10,1... | collective-permute-start | bytes 786440 | tf_op jit(solution)/shard_map/ppermute | solution.py:13
  65.9 13.8 %collective-permute-start.7 = (bf16[256,512]{1,0:T(8,128)(2,1)}, bf16[256,512]{1,0:T(8,128)(2,1)}, u32[]{:S(2)}, u32[]{:S(2)}) collective-permute-start(bf16[256,512]{1,0:T(8,128)(2,1)} %get-tuple-element.13), channel_id=1, source_target_pairs={{1,0},{2,1},{3,2},{4,3},{5,4},{6,5},{7,6},{8,7},{9,8},{10,9},{11,1... | collective-permute-start | bytes 786440 | tf_op jit(solution)/shard_map/ppermute | solution.py:13
  73.6 10.6 %collective-permute-start.8 = (bf16[256,512]{1,0:T(8,128)(2,1)}, bf16[256,512]{1,0:T(8,128)(2,1)}, u32[]{:S(2)}, u32[]{:S(2)}) collective-permute-start(bf16[256,512]{1,0:T(8,128)(2,1)} %get-tuple-element.12), channel_id=1, source_target_pairs={{2,0},{3,1},{4,2},{5,3},{6,4},{7,5},{8,6},{9,7},{10,8},{11,9},{12,... | collective-permute-start | bytes 786440 | tf_op jit(solution)/shard_map/ppermute | solution.py:13
  74.9 10.1 %collective-permute-start.9 = (bf16[256,512]{1,0:T(8,128)(2,1)}, bf16[256,512]{1,0:T(8,128)(2,1)}, u32[]{:S(2)}, u32[]{:S(2)}) collective-permute-start(bf16[256,512]{1,0:T(8,128)(2,1)} %get-tuple-element.11), channel_id=1, source_target_pairs={{3,0},{4,1},{5,2},{6,3},{7,4},{8,5},{9,6},{10,7},{11,8},{12,9},{13... | collective-permute-start | bytes 786440 | tf_op jit(solution)/shard_map/ppermute | solution.py:13
  96.3 16.1 %all-to-all-start.1 = ((bf16[32,2,1024]{2,1,0:T(2,128)(2,1)}), bf16[32,2,1024]{2,1,0:T(2,128)(2,1)S(1)}, u32[]{:S(2)}, u32[]{:S(2)}) async-start(bf16[32,2,1024]{2,1,0:T(2,128)(2,1)} %reshape.605), calls=%async_computation.1 | async-start | bytes 262144 | tf_op jit(solution)/shard_map/all_to_all | solution.py:107
  104.1 50.9 %all-gather.4.cloned.1.call-start = ((), (), s32[]{:S(2)}) async-start(), calls=%async_computation.4 | async-start | bytes 1572864 | tf_op jit(solution)/shard_map/all_gather | solution.py:156
  142.0 2.8 %copy-start.1 = (bf16[64,4096]{1,0:T(8,128)(2,1)S(1)}, bf16[64,4096]{1,0:T(8,128)(2,1)}, u32[]{:S(2)}) copy-start(bf16[64,4096]{1,0:T(8,128)(2,1)} %reshape.592) | copy-start | bytes 1572868
  142.0 3.2 %copy-start.2 = (bf16[1,4096,384]{2,1,0:T(8,128)(2,1)S(1)}, bf16[1,4096,384]{2,1,0:T(8,128)(2,1)}, u32[]{:S(2)}) copy-start(bf16[1,4096,384]{2,1,0:T(8,128)(2,1)} %param.26) | copy-start | bytes 9437188
  155.0 29.0 %copy-start.4 = (bf16[4,4096]{1,0:T(4,128)(2,1)S(1)}, bf16[4,4096]{1,0:T(4,128)(2,1)}, u32[]{:S(2)}) copy-start(bf16[4,4096]{1,0:T(4,128)(2,1)} %param.20) | copy-start | bytes 98308
  155.0 29.0 %copy-start.7 = (f32[64,8]{0,1:T(8,128)S(1)}, f32[64,8]{0,1:T(8,128)}, u32[]{:S(2)}) copy-start(f32[64,8]{0,1:T(8,128)} %get-tuple-element.5) | copy-start | bytes 6148
  159.6 22.4 %all-to-all-start.3 = ((bf16[16,4,4096]{2,1,0:T(4,128)(2,1)}), bf16[16,4,4096]{2,1,0:T(4,128)(2,1)}, u32[]{:S(2)}, u32[]{:S(2)}) async-start(bf16[16,4,4096]{2,1,0:T(4,128)(2,1)} %copy.44), calls=%async_computation.3 | async-start | bytes 1048576 | tf_op jit(solution)/shard_map/all_to_all | solution.py:158
Sparse Core Ops, SparseCore 0:
  147.4 7.5 all-gather.3
